TPU v7x, 32 devices: a whole 2x2x4 slice. The times are simulated.
32 devices in a mesh: head: 8 (over y, x, core), seq: 4 (over z).
Axes of the slice: x: 2, y: 2, z: 4, core: 2. Of those that a mesh axis runs over, the one named last changes fastest.
Arguments:
- query_rows: bfloat16 [512, 16384], P('seq', 'head'), may hold values from -512 to 512
- key_rows: bfloat16 [512, 1024], P('seq'), may hold values from -32 to 32
- value_rows: bfloat16 [512, 1024], P('seq'), may hold values from -6 to 6
- positions: int32 [512], P('seq'), may hold values from 0 to 511, as said below
Outputs:
- attended: bfloat16 [512, 16384], P('seq', 'head')
- hessian: float32 [16384, 16384], P('head', 'seq')
Inputs may be any that keep to these rules, and one draw needn't show every extreme that they name: Each aligned block of 4 spans of 128 tokens is one sequence; each span holds 128 consecutive ascending positions starting at a multiple of 128, and the sequence's spans together hold every position 0 to 511 once.
All inputs are finite; a program needn't handle non-finite values.
Results may differ from a plain program's by a relative error of at most 0.0037.
Values may be sent and summed in bfloat16 or wider, within the bound.
A program may use at most 128 MiB of HBM per device.

v0:
```python
import jax
import jax.numpy as jnp
from jax import lax
from jax.sharding import PartitionSpec as P

HEADS = 128
KVH = 8
HD = 128
SPANS = 4


def from_partner(value, axis, stride):
    mask = 2**stride
    pairs = [(source, source ^ mask) for source in range(lax.axis_size(axis))]
    return lax.ppermute(value, axis, pairs)


def spread(x, axis, root):
    mine = lax.axis_index(axis) == root
    return lax.psum(jnp.where(mine, x, jnp.zeros_like(x)), axis)


def attend_block(queries, key_block, value_block, visible, local_heads, local_tokens, score_scale):
    scores = jnp.dot(queries, key_block.T, preferred_element_type=jnp.float32) * score_scale
    scores = scores.reshape(local_heads, local_tokens, key_block.shape[0])
    masked = jnp.where(visible[None], scores, -jnp.inf)
    row_top = jnp.max(masked, axis=2, keepdims=True)
    weights = jnp.exp(masked - row_top)
    weight_sum = jnp.sum(weights, axis=2, keepdims=True)
    mixed = jnp.dot(
        weights.astype(jnp.bfloat16).reshape(local_heads * local_tokens, key_block.shape[0]),
        value_block,
        preferred_element_type=jnp.float32,
    )
    return mixed.reshape(local_heads, local_tokens, HD) / weight_sum


def on_device(query_rows, key_rows, value_rows, positions):
    local_tokens = query_rows.shape[0]
    local_heads = query_rows.shape[1] // HD
    group_size = HEADS // KVH
    score_scale = HD ** (-0.5)
    head_index = lax.axis_index("head")
    span_index = lax.axis_index("seq")
    seq_devices = lax.axis_size("seq")
    head_devices = lax.axis_size("head")
    key_head = head_index * local_heads // group_size
    key_slice = lax.dynamic_slice_in_dim(key_rows, key_head * HD, HD, 1)
    value_slice = lax.dynamic_slice_in_dim(value_rows, key_head * HD, HD, 1)
    queries = jnp.transpose(query_rows.reshape(local_tokens, local_heads, HD), (1, 0, 2))
    queries = queries.reshape(local_heads * local_tokens, HD)
    key_block, value_block, place_block = (key_slice, value_slice, positions)
    for bit in range(SPANS.bit_length() - 1):
        other_keys, other_values, other_places = from_partner(
            (key_block, value_block, place_block), "seq", bit
        )
        key_block = jnp.concatenate([key_block, other_keys], axis=0)
        value_block = jnp.concatenate([value_block, other_values], axis=0)
        place_block = jnp.concatenate([place_block, other_places], axis=0)
    visible = place_block[None, :] <= positions[:, None]
    outcome = attend_block(
        queries, key_block, value_block, visible, local_heads, local_tokens, score_scale
    )
    attended = (
        jnp.transpose(outcome, (1, 0, 2))
        .reshape(local_tokens, local_heads * HD)
        .astype(jnp.bfloat16)
    )
    row_operand = lax.all_gather(attended, "seq", axis=0, tiled=True)
    root_count = head_devices // seq_devices
    column_parts = []
    for offset in range(root_count):
        column_parts.append(spread(row_operand, "head", span_index * root_count + offset))
    columns = jnp.concatenate(column_parts, axis=1)
    hessian = lax.dot_general(
        row_operand, columns, (((0,), (0,)), ((), ())), preferred_element_type=jnp.float32
    )
    return (attended, hessian)


def solution(mesh):
    placed = (P("seq", "head"), P("seq", None), P("seq", None), P("seq"))
    return jax.shard_map(
        on_device,
        mesh=mesh,
        in_specs=placed,
        out_specs=(P("seq", "head"), P("head", "seq")),
        check_vma=False,
    )
```

profile of v0, /device:TPU:25, one launch (start us, length us, event | category | flops | bytes accessed | tf_op | source)
XLA Modules:
  0.0 184.5 jit_solution(7501032044831482604)
XLA Ops:
  7.2 0.0 copy-start
  7.2 0.0 copy-start.3
  7.2 0.0 all-gather.2.cloned.1.call-start
  7.2 0.2 collective-permute-start
  7.5 0.6 copy-done
  8.1 0.1 copy.18
  8.2 0.7 collective-permute-start.4
  9.0 0.9 collective-permute-done
  9.9 0.7 pad_add_fusion.1
  10.5 0.1 collective-permute-start.1
  10.6 0.8 constant_dynamic-slice_fusion.1
  11.3 0.1 collective-permute-start.2
  11.5 1.3 copy.12
  12.8 0.3 copy.13
  13.1 0.8 collective-permute-done.1
  13.8 0.0 copy-done.3
  13.9 0.1 broadcast_compare_fusion
  14.0 0.1 collective-permute-done.2
  14.1 2.4 %collective-permute-start.3 = (bf16[256,128]{1,0:T(8,128)(2,1)S(1)}, bf16[256,128]{1,0:T(8,128)(2,1)S(1)}, u32[]{:S(2)}, u32[]{:S(2)}) collective-permute-start(bf16[256,128]{1,0:T(8,128)(2,1)S(1)} %pad_maximum_fusion), channel_id=1, source_target_pairs={{0,2},{1,3},{2,0},{3,1},{4,6},{5,7},{6,4},{7,5},{8,10},{9,11},{10,... | collective-permute-start | bytes 196616 | tf_op jit(solution)/shard_map/ppermute | solution.py:15
  16.5 0.0 collective-permute-done.4
  16.5 0.1 collective-permute-start.5
  16.6 2.3 %collective-permute-done.3 = bf16[256,128]{1,0:T(8,128)(2,1)S(1)} collective-permute-done((bf16[256,128]{1,0:T(8,128)(2,1)S(1)}, bf16[256,128]{1,0:T(8,128)(2,1)S(1)}, u32[]{:S(2)}, u32[]{:S(2)}) %collective-permute-start.3) | collective-permute-done | bytes 65568 | tf_op jit(solution)/shard_map/ppermute | solution.py:15
  18.8 0.3 broadcast_in_dim.19
  19.1 1.0 fusion.20
  20.1 0.7 fusion.4
  20.8 2.5 %copy.17 = bf16[2048,512]{1,0:T(8,128)(2,1)} copy(bf16[2048,512]{0,1:T(8,128)(2,1)S(1)} %get-tuple-element.11) | data formatting | bytes 4194304 | tf_op jit(solution)/shard_map/dot_general | solution.py:30
  23.3 0.0 collective-permute-done.5
  23.3 3.2 %fusion.7 = bf16[128,16,128]{0,2,1:T(8,128)(2,1)} fusion(bf16[16,128,512]{2,1,0:T(8,128)(2,1)} %bitcast.28, f32[128,16]{0,1:T(8,128)S(1)} %bitcast.34, bf16[256,128]{0,1:T(8,128)(2,1)S(1)} %collective-permute-done.5, bf16[128,128]{0,1:T(8,128)(2,1)S(1)} %collective-permute-done.4, bf16[128,128]{0,1:T(8,128)(2,1)S(1)} %copy.18), kind=kOutput, calls=%fused_computation.12 | convolution fusion | flops 269352960 | bytes 2760704 | tf_op jit(solution)/shard_map/dot_general | solution.py:30
  26.5 0.0 all-gather.2.cloned.1.call-update
  26.5 0.0 all-reduce.3.cloned.1.call-start
  26.6 48.5 %all-gather.2.cloned.1.call-done = bf16[512,2048]{0,1:T(8,128)(2,1)} async-done(((bf16[128,2048]{0,1:T(8,128)(2,1)}), bf16[512,2048]{0,1:T(8,128)(2,1)}) %all-gather.2.cloned.1.call-update) | async-done | bytes 2097168 | tf_op jit(solution)/shard_map/all_gather | solution.py:69
  75.0 3.9 %broadcast_select_fusion.1 = (bf16[512,2048]{0,1:T(8,128)(2,1)}, bf16[512,2048]{0,1:T(8,128)(2,1)}) fusion(bf16[512,2048]{0,1:T(8,128)(2,1)} %all-gather.2.cloned.1.call-done, pred[]{:T(512)S(6)} %eq.6, pred[]{:T(512)S(6)} %eq.7), kind=kLoop, calls=%fused_computation.9 | loop fusion | flops 2097152 | bytes 6291458 | tf_op jit(solution)/shard_map/jit(_where)/select_n | solution.py:20
  78.9 0.0 copy-start.2
  78.9 0.0 copy-start.1
  78.9 0.0 all-reduce.3.cloned.1.call-update
  78.9 1.0 copy-done.2
  79.9 1.0 copy.16
  80.9 79.7 %all-reduce.3.cloned.1.call-done = (bf16[512,2048]{0,1:T(8,128)(2,1)}, bf16[512,2048]{0,1:T(8,128)(2,1)}) async-done(((bf16[512,2048]{0,1:T(8,128)(2,1)}, bf16[512,2048]{0,1:T(8,128)(2,1)}), (bf16[512,2048]{0,1:T(8,128)(2,1)}, bf16[512,2048]{0,1:T(8,128)(2,1)})) %all-reduce.3.cloned.1.call-update) | async-done | bytes 4194320 | tf_op jit(solution)/shard_map/psum | solution.py:20
  160.6 0.0 copy-done.1
  160.6 17.1 %fusion = f32[2048,4096]{1,0:T(8,128)} fusion(bf16[512,2048]{0,1:T(8,128)(2,1)S(1)} %copy-done.1, bf16[512,2048]{0,1:T(8,128)(2,1)} %get-tuple-element.8, bf16[512,2048]{0,1:T(8,128)(2,1)} %get-tuple-element.9), kind=kOutput, calls=%fused_computation | convolution fusion | flops 8598323200 | bytes 39845888 | tf_op jit(solution)/shard_map/dot_general | solution.py:75
  (4 shorter events, 0.0 us)
Async XLA Ops:
  7.2 1.0 copy-start
  7.2 6.7 %copy-start.3 = (s32[128]{0:T(128)S(1)}, s32[128]{0:T(128)}, u32[]{:S(2)}) copy-start(s32[128]{0:T(128)} %param.7) | copy-start | bytes 1540
  7.2 67.8 %all-gather.2.cloned.1.call-start = ((), (), s32[]{:S(2)}) async-start(), calls=%async_computation | async-start | bytes 2621440 | tf_op jit(solution)/shard_map/all_gather | solution.py:69
  7.2 2.6 %collective-permute-start = (s32[128]{0:T(128)}, s32[128]{0:T(128)S(1)}, u32[]{:S(2)}, u32[]{:S(2)}) collective-permute-start(s32[128]{0:T(128)} %param.7), channel_id=1, source_target_pairs={{0,1},{1,0},{2,3},{3,2},{4,5},{5,4},{6,7},{7,6},{8,9},{9,8},{10,11... | collective-permute-start | bytes 1544 | tf_op jit(solution)/shard_map/ppermute | solution.py:15
  8.2 8.2 %collective-permute-start.4 = (bf16[128,128]{0,1:T(8,128)(2,1)S(1)}, bf16[128,128]{0,1:T(8,128)(2,1)S(1)}, u32[]{:S(2)}, u32[]{:S(2)}) collective-permute-start(bf16[128,128]{0,1:T(8,128)(2,1)S(1)} %copy.18), channel_id=1, source_target_pairs={{0,1},{1,0},{2,3},{3,2},{4,5},{5,4},{6,7},{7,6},{8,9},{9,8},{10,11... | collective-permute-start | bytes 98312 | tf_op jit(solution)/shard_map/ppermute | solution.py:15
  10.5 3.3 %collective-permute-start.1 = (s32[256]{0:T(256)S(1)}, s32[256]{0:T(256)S(1)}, u32[]{:S(2)}, u32[]{:S(2)}) collective-permute-start(s32[256]{0:T(256)S(1)} %pad_add_fusion.1), channel_id=1, source_target_pairs={{0,2},{1,3},{2,0},{3,1},{4,6},{5,7},{6,4},{7,5},{8,10},{9,11},{10,... | collective-permute-start | bytes 3080 | tf_op jit(solution)/shard_map/ppermute | solution.py:15
  11.3 2.8 %collective-permute-start.2 = (bf16[128,128]{1,0:T(8,128)(2,1)S(1)}, bf16[128,128]{1,0:T(8,128)(2,1)S(1)}, u32[]{:S(2)}, u32[]{:S(2)}) collective-permute-start(bf16[128,128]{1,0:T(8,128)(2,1)S(1)} %constant_dynamic-slice_fusion.1), channel_id=1, source_target_pairs={{0,1},{1,0},{2,3},{3,2},{4,5},{5,4},{6,7},{7,6},{8,9},{9,8},{10,11... | collective-permute-start | bytes 98312 | tf_op jit(solution)/shard_map/ppermute | solution.py:15
  14.1 4.7 %collective-permute-start.3 = (bf16[256,128]{1,0:T(8,128)(2,1)S(1)}, bf16[256,128]{1,0:T(8,128)(2,1)S(1)}, u32[]{:S(2)}, u32[]{:S(2)}) collective-permute-start(bf16[256,128]{1,0:T(8,128)(2,1)S(1)} %pad_maximum_fusion), channel_id=1, source_target_pairs={{0,2},{1,3},{2,0},{3,1},{4,6},{5,7},{6,4},{7,5},{8,10},{9,11},{10,... | collective-permute-start | bytes 196616 | tf_op jit(solution)/shard_map/ppermute | solution.py:15
  16.5 6.8 %collective-permute-start.5 = (bf16[256,128]{0,1:T(8,128)(2,1)S(1)}, bf16[256,128]{0,1:T(8,128)(2,1)S(1)}, u32[]{:S(2)}, u32[]{:S(2)}) collective-permute-start(bf16[256,128]{0,1:T(8,128)(2,1)S(1)} %pad_maximum_fusion.1), channel_id=1, source_target_pairs={{0,2},{1,3},{2,0},{3,1},{4,6},{5,7},{6,4},{7,5},{8,10},{9,11},{10,... | collective-permute-start | bytes 196616 | tf_op jit(solution)/shard_map/ppermute | solution.py:15
  26.5 134.1 %all-reduce.3.cloned.1.call-start = ((), (), s32[]{:S(2)}) async-start(), calls=%async_computation.1 | async-start | bytes 8388608 | tf_op jit(solution)/shard_map/psum | solution.py:20
  78.9 1.0 copy-start.2
  78.9 81.7 %copy-start.1 = (bf16[512,2048]{0,1:T(8,128)(2,1)S(1)}, bf16[512,2048]{0,1:T(8,128)(2,1)}, u32[]{:S(2)}) copy-start(bf16[512,2048]{0,1:T(8,128)(2,1)} %all-gather.2.cloned.1.call-done) | copy-start | bytes 6291460
Sparse Core Ops, SparseCore 0:
  26.6 48.3 all-gather.1
  79.0 81.5 all-reduce.2
where the time goes:
time: 187 us; the launch traced here: 185 us
  waiting for transfers between devices  132 us (71%)
  matrix products  21.2 us (11%)
  between operations  14.1 us (8%)
  local copies, waits for them, and re-layouts  7.94 us (4%)
  other arithmetic  5.39 us (3%)
  starting transfers between devices  3.66 us (2%)
    psum x1, waiting for transfers between devices, spread(): return lax.psum(jnp.where(mine, x, jnp.zeros_like(x)), axis)  79.7 us
    all_gather x1, waiting for transfers between devices, on_device(): row_operand = lax.all_gather(attended, 'seq', axis=0, tiled=True)  48.5 us
    dot_general x1, matrix products, on_device(): lax.dot_general(row_operand, columns, (((0,), (0,)), ((), ())), preferred...  17.1 us
    unnamed x11, local copies, waits for them, and re-layouts  4.11 us
    ppermute x6, waiting for transfers between devices, from_partner(): return lax.ppermute(value, axis, pairs)  4.04 us
    select_n x1, other arithmetic, spread(): return lax.psum(jnp.where(mine, x, jnp.zeros_like(x)), axis)  3.89 us
  transfers between devices with their start and end apart: 8, of which 6 were waited for; matrix products, arithmetic and copies ran while one was open for 5% of the time, Pallas kernels for 0%

commit v1 on v0

v1 whole, which is shorter than its diff:
```python
import functools

import jax
import jax.numpy as jnp
from jax import lax
from jax.experimental import pallas as pl
from jax.experimental.pallas import tpu as pltpu
from jax.sharding import PartitionSpec as P

HEADS = 128
KVH = 8
HD = 128
SPANS = 4
MESH = pl.DeviceIdType.MESH


def exchange_kernel(
    seq_devices, head_devices, chunks,
    q_ref, k_ref, v_ref, pos_ref, rows_ref, cols_ref,
    kbuf, vbuf, pbuf,
    kv_send, kv_recv, line_send, line_recv, tree_send, tree_recv, lane_send, lane_recv,
):
    tokens, width = q_ref.shape
    lanes = head_devices // seq_devices
    bits = seq_devices.bit_length() - 1
    chunk_width = width // chunks
    chunk_heads = chunk_width // HD
    score_scale = HD ** (-0.5)
    head = lax.axis_index("head")
    span = lax.axis_index("seq")
    node, lane = head // lanes, head % lanes
    group = (span // SPANS) * SPANS
    place = span % SPANS

    def flip(bit):
        has = (node // 2**bit) % 2
        return (node + (1 - 2 * has) * 2**bit) * lanes + lane

    far = [(node // 2**bit + span // 2**bit) % 2 for bit in range(bits)]
    above = [sum(far[bit:]) for bit in range(bits)]
    root = above[0] == 0
    not_root = above[0] > 0

    def peer(step):
        return group + (place + step) % SPANS

    def mate(step):
        return node * lanes + (lane + step) % lanes

    barrier = pltpu.get_barrier_semaphore()
    count = 0
    for step in range(1, SPANS):
        pl.semaphore_signal(barrier, inc=1, device_id={"seq": peer(step)}, device_id_type=MESH)
        count += 1
    for bit in range(bits):
        pl.semaphore_signal(barrier, inc=1, device_id={"head": flip(bit)}, device_id_type=MESH)
        count += 1
    for step in range(1, lanes):
        pl.semaphore_signal(barrier, inc=1, device_id={"head": mate(step)}, device_id_type=MESH)
        count += 1
    if seq_devices > SPANS:
        @pl.when(span > 0)
        def _():
            pl.semaphore_signal(barrier, inc=1, device_id={"seq": span - 1}, device_id_type=MESH)

        @pl.when(span < seq_devices - 1)
        def _():
            pl.semaphore_signal(barrier, inc=1, device_id={"seq": span + 1}, device_id_type=MESH)

        @pl.when(span > 0)
        def _():
            pl.semaphore_wait(barrier, 1)

        @pl.when(span < seq_devices - 1)
        def _():
            pl.semaphore_wait(barrier, 1)

    pl.semaphore_wait(barrier, count)
    key_head = head * (width // HD) // (HEADS // KVH)
    key_columns = pl.ds(pl.multiple_of(key_head * HD, HD), HD)

    def kv_copies(step):
        copies = []
        for which, (src, dst) in enumerate((
            (k_ref.at[:, key_columns], kbuf.at[place]),
            (v_ref.at[:, key_columns], vbuf.at[place]),
            (pos_ref, pbuf.at[place]),
        )):
            copies.append(pltpu.make_async_remote_copy(
                src_ref=src, dst_ref=dst,
                send_sem=kv_send.at[which, step - 1], recv_sem=kv_recv.at[which, step - 1],
                device_id={"seq": peer(step)}, device_id_type=MESH,
            ))
        return copies

    def kv_arrivals(step):
        source = (place + SPANS - step) % SPANS
        copies = []
        for which, (src, dst) in enumerate((
            (k_ref.at[:, key_columns], kbuf.at[source]),
            (v_ref.at[:, key_columns], vbuf.at[source]),
            (pos_ref, pbuf.at[source]),
        )):
            copies.append(pltpu.make_async_remote_copy(
                src_ref=src, dst_ref=dst,
                send_sem=kv_send.at[which, step - 1], recv_sem=kv_recv.at[which, step - 1],
                device_id={"seq": peer(step)}, device_id_type=MESH,
            ))
        return copies

    for step in range(1, SPANS):
        for copy in kv_copies(step):
            copy.start()
    kbuf[place] = k_ref[:, key_columns]
    vbuf[place] = v_ref[:, key_columns]
    pbuf[place] = pos_ref[...]

    def row_chunk(block, part):
        return (
            pl.ds(pl.multiple_of(block * tokens, tokens), tokens),
            pl.ds(pl.multiple_of(part * chunk_width, chunk_width), chunk_width),
        )

    def col_chunk(of_lane, block, part):
        return (
            pl.ds(pl.multiple_of(block * tokens, tokens), tokens),
            pl.ds(pl.multiple_of(of_lane * width + part * chunk_width, chunk_width), chunk_width),
        )

    def line_copy(way, block, part):
        where = rows_ref.at[row_chunk(block, part)]
        return pltpu.make_async_remote_copy(
            src_ref=where, dst_ref=where,
            send_sem=line_send.at[way, block, part], recv_sem=line_recv.at[block, part],
            device_id={"seq": span + 1 - 2 * way}, device_id_type=MESH,
        )

    def tree_copy(bit, block, part, source):
        return pltpu.make_async_remote_copy(
            src_ref=source, dst_ref=cols_ref.at[col_chunk(lane, block, part)],
            send_sem=tree_send.at[bit, block, part], recv_sem=tree_recv.at[block, part],
            device_id={"head": flip(bit)}, device_id_type=MESH,
        )

    def lane_copy(step, of_lane, block, part, source):
        return pltpu.make_async_remote_copy(
            src_ref=source, dst_ref=cols_ref.at[col_chunk(of_lane, block, part)],
            send_sem=lane_send.at[step - 1, block, part],
            recv_sem=lane_recv.at[step - 1, block, part],
            device_id={"head": mate(step)}, device_id_type=MESH,
        )

    def spread(block, part, source):
        for bit in range(bits):
            @pl.when(above[bit] == 0)
            def _():
                tree_copy(bit, block, part, source).start()
        for step in range(1, lanes):
            lane_copy(step, lane, block, part, source).start()

    def on_row(block, part, up, down):
        @pl.when(up)
        def _():
            line_copy(0, block, part).start()

        @pl.when(down)
        def _():
            line_copy(1, block, part).start()

        @pl.when(root)
        def _():
            spread(block, part, rows_ref.at[row_chunk(block, part)])
            cols_ref[col_chunk(lane, block, part)] = rows_ref[row_chunk(block, part)]

    has_up = span < seq_devices - 1
    has_down = span > 0

    for step in range(1, SPANS):
        for copy in kv_arrivals(step):
            copy.wait_recv()

    keys = kbuf[...].reshape(SPANS * tokens, HD)
    values = vbuf[...].reshape(SPANS * tokens, HD)
    key_places = jnp.concatenate([pbuf[j] for j in range(SPANS)], axis=1)
    query_places = jnp.broadcast_to(pos_ref[0:1, 0:1], (tokens, 1)) + lax.broadcasted_iota(
        jnp.int32, (tokens, 1), 0
    )
    visible = key_places <= query_places

    def compute(part, carry):
        pieces = []
        for h in range(chunk_heads):
            columns = pl.ds(pl.multiple_of(part * chunk_width + h * HD, HD), HD)
            queries = q_ref[:, columns]
            scores = lax.dot_general(
                queries, keys, (((1,), (1,)), ((), ())), preferred_element_type=jnp.float32
            ) * score_scale
            masked = jnp.where(visible, scores, -jnp.inf)
            row_top = jnp.max(masked, axis=1, keepdims=True)
            weights = jnp.exp(masked - row_top)
            weight_sum = jnp.sum(weights, axis=1, keepdims=True)
            mixed = jnp.dot(
                weights.astype(jnp.bfloat16), values, preferred_element_type=jnp.float32
            )
            pieces.append((mixed / weight_sum).astype(jnp.bfloat16))
        rows_ref[row_chunk(span, part)] = jnp.concatenate(pieces, axis=1)
        on_row(span, part, has_up, has_down)
        return carry

    lax.fori_loop(0, chunks, compute, 0)

    def relay(item, carry):
        back, part = item // chunks, item % chunks
        reach = back + 1

        @pl.when(reach <= span)
        def _():
            block = span - reach
            line_copy(0, block, part).wait_recv()
            on_row(block, part, has_up, False)

        @pl.when(span + reach < seq_devices)
        def _():
            block = span + reach
            line_copy(1, block, part).wait_recv()
            on_row(block, part, False, has_down)

        def from_parent(block):
            source = cols_ref.at[col_chunk(lane, block, part)]
            tree_copy(0, block, part, source).wait_recv()
            spread(block, part, source)

        @pl.when(not_root)
        def _():
            @pl.when(back <= span)
            def _():
                from_parent(span - back)

            @pl.when(jnp.logical_and(back > 0, span + back < seq_devices))
            def _():
                from_parent(span + back)

        return carry

    lax.fori_loop(0, seq_devices * chunks, relay, 0)

    def drain(item, carry):
        block, part = item // chunks, item % chunks
        source = cols_ref.at[col_chunk(lane, block, part)]

        @pl.when(jnp.logical_and(has_up, block <= span))
        def _():
            line_copy(0, block, part).wait_send()

        @pl.when(jnp.logical_and(has_down, block >= span))
        def _():
            line_copy(1, block, part).wait_send()

        for bit in range(bits):
            @pl.when(above[bit] == 0)
            def _():
                tree_copy(bit, block, part, source).wait_send()
        for step in range(1, lanes):
            lane_copy(step, lane, block, part, source).wait_send()
            lane_copy(step, (lane + lanes - step) % lanes, block, part, source).wait_recv()
        return carry

    lax.fori_loop(0, seq_devices * chunks, drain, 0)
    for step in range(1, SPANS):
        for copy in kv_copies(step):
            copy.wait_send()


def on_device(query_rows, key_rows, value_rows, positions):
    tokens, width = query_rows.shape
    seq_devices = lax.axis_size("seq")
    head_devices = lax.axis_size("head")
    lanes = head_devices // seq_devices
    bits = seq_devices.bit_length() - 1
    chunks = max(1, width // (4 * HD))
    vmem = pl.BlockSpec(memory_space=pltpu.VMEM)
    dma = pltpu.SemaphoreType.DMA
    rows, cols = pl.pallas_call(
        functools.partial(exchange_kernel, seq_devices, head_devices, chunks),
        out_shape=(
            jax.ShapeDtypeStruct((seq_devices * tokens, width), jnp.bfloat16),
            jax.ShapeDtypeStruct((seq_devices * tokens, lanes * width), jnp.bfloat16),
        ),
        in_specs=[vmem] * 4,
        out_specs=(vmem, vmem),
        scratch_shapes=[
            pltpu.VMEM((SPANS, tokens, HD), jnp.bfloat16),
            pltpu.VMEM((SPANS, tokens, HD), jnp.bfloat16),
            pltpu.VMEM((SPANS, 1, tokens), jnp.int32),
            dma((3, SPANS - 1)),
            dma((3, SPANS - 1)),
            dma((2, seq_devices, chunks)),
            dma((seq_devices, chunks)),
            dma((bits, seq_devices, chunks)),
            dma((seq_devices, chunks)),
            dma((lanes - 1, seq_devices, chunks)),
            dma((lanes - 1, seq_devices, chunks)),
        ],
        compiler_params=pltpu.CompilerParams(collective_id=0, has_side_effects=True),
        name="attend_exchange",
    )(query_rows, key_rows, value_rows, positions.reshape(1, tokens))
    attended = lax.dynamic_slice_in_dim(rows, lax.axis_index("seq") * tokens, tokens, 0)
    hessian = lax.dot_general(
        rows, cols, (((0,), (0,)), ((), ())), preferred_element_type=jnp.float32
    )
    return (attended, hessian)


def solution(mesh):
    placed = (P("seq", "head"), P("seq", None), P("seq", None), P("seq"))
    return jax.shard_map(
        on_device,
        mesh=mesh,
        in_specs=placed,
        out_specs=(P("seq", "head"), P("head", "seq")),
        check_vma=False,
    )
```

time: 187 us -> 90.3 us (0.48)
  waiting for transfers between devices: 132 us -> 0 us
  Pallas kernels: 0 us -> 68.3 us
  between operations: 14.1 us -> 0.64 us
  local copies, waits for them, and re-layouts: 7.94 us -> 1.89 us
  other arithmetic: 5.39 us -> 0 us
  starting transfers between devices: 3.66 us -> 0 us
  matrix products: 21.2 us -> 18.8 us
    psum x1 -> x0, waiting for transfers between devices: 79.7 us -> none  [spread(): return lax.psum(jnp.where(mine, x, jnp.zeros_like(x)), axis)]
    pallas_call x0 -> x1, Pallas kernels: none -> 68.3 us  [on_device(): pl.pallas_call(functools.partial(exchange_kernel, seq_devices, head_devic...]
    all_gather x1 -> x0, waiting for transfers between devices: 48.5 us -> none  [on_device(): row_operand = lax.all_gather(attended, 'seq', axis=0, tiled=True)]
    unnamed x11 -> x0, local copies, waits for them, and re-layouts: 4.11 us -> none
    ppermute x6 -> x0, waiting for transfers between devices: 4.04 us -> none  [from_partner(): return lax.ppermute(value, axis, pairs)]
    select_n x1 -> x0, other arithmetic: 3.89 us -> none  [spread(): return lax.psum(jnp.where(mine, x, jnp.zeros_like(x)), axis)]
    ppermute x6 -> x0, starting transfers between devices: 3.58 us -> none  [from_partner(): return lax.ppermute(value, axis, pairs)]
    dot_general x1 -> x0, local copies, waits for them, and re-layouts: 2.5 us -> none  [attend_block(): jnp.dot(weights.astype(jnp.bfloat16).reshape(local_heads * local_tokens,...]
  transfers between devices with their start and end apart: 8 -> 0, of which waited for: 6 -> 0; matrix products, arithmetic and copies ran while one was open for 5% -> 0% of each run, Pallas kernels for 0% -> 0%
where the time goes in v1:
time: 90.3 us; the launch traced here: 89.6 us
  Pallas kernels  68.3 us (76%)
  matrix products  18.8 us (21%)
  local copies, waits for them, and re-layouts  1.89 us (2%)
    pallas_call x1, Pallas kernels, on_device(): pl.pallas_call(functools.partial(exchange_kernel, seq_devices, head_devic...  68.3 us
    dot_general x1, matrix products, on_device(): lax.dot_general(rows, cols, (((0,), (0,)), ((), ())), preferred_element_t...  18.8 us
    dynamic_slice x1, local copies, waits for them, and re-layouts, on_device(): lax.dynamic_slice_in_dim(rows, lax.axis_index('seq') * tokens, tokens, 0)  1.89 us

profile of v1, /device:TPU:25, one launch (start us, length us, event | category | flops | bytes accessed | tf_op | source)
XLA Modules:
  0.0 89.6 jit_solution(10459330737189842547)
XLA Ops:
  0.6 68.3 %attend_exchange.1 = (bf16[512,2048]{1,0:T(8,128)(2,1)}, bf16[512,4096]{1,0:T(8,128)(2,1)}) custom-call(bf16[128,2048]{1,0:T(8,128)(2,1)} %q_ref.1, bf16[128,1024]{1,0:T(8,128)(2,1)} %k_ref.1, bf16[128,1024]{1,0:T(8,128)(2,1)} %v_ref.1, s32[1,128]{1,0:T(1,128)} %bitcast.3), custom_call_target="tpu_custom_call" | custom-call | tf_op jit(solution)/shard_map/attend_exchange/pallas_call | solution.py:283
  68.9 1.9 %constant_dynamic-slice_fusion = bf16[128,2048]{1,0:T(8,128)(2,1)} fusion(bf16[512,2048]{1,0:T(8,128)(2,1)} %get-tuple-element.4, s32[]{:T(128)S(6)} %select_n.3), kind=kLoop, calls=%fused_computation | loop fusion | bytes 1048580 | tf_op jit(solution)/shard_map/dynamic_slice | solution.py:307
  70.8 18.8 %fusion = f32[2048,4096]{1,0:T(8,128)} fusion(bf16[512,2048]{1,0:T(8,128)(2,1)} %get-tuple-element.4, bf16[512,4096]{1,0:T(8,128)(2,1)} %get-tuple-element.5), kind=kOutput, calls=%fused_computation.1 | convolution fusion | flops 8589934592 | bytes 39845888 | tf_op jit(solution)/shard_map/dot_general | solution.py:308

commit v2 on v1

--- a/solution.py
+++ b/solution.py
@@ -11,13 +11,15 @@
 KVH = 8
 HD = 128
 SPANS = 4
+CHUNK_HEADS = 4
+TILE = 512
 MESH = pl.DeviceIdType.MESH
 
 
 def exchange_kernel(
     seq_devices, head_devices, chunks,
-    q_ref, k_ref, v_ref, pos_ref, rows_ref, cols_ref,
-    kbuf, vbuf, pbuf,
+    q_ref, k_ref, v_ref, pos_ref, attended_ref, turned_ref, cols_ref,
+    rows_ref, kbuf, vbuf, pbuf,
     kv_send, kv_recv, line_send, line_recv, tree_send, tree_recv, lane_send, lane_recv,
 ):
     tokens, width = q_ref.shape
@@ -38,6 +40,7 @@
 
     far = [(node // 2**bit + span // 2**bit) % 2 for bit in range(bits)]
     above = [sum(far[bit:]) for bit in range(bits)]
+    below = [sum(far[: bit + 1]) for bit in range(bits)]
     root = above[0] == 0
     not_root = above[0] > 0
 
@@ -150,9 +153,13 @@
             device_id={"head": mate(step)}, device_id_type=MESH,
         )
 
+    def sends(bit, block, part):
+        turn = (block + part) % 2
+        return turn * above[bit] + (1 - turn) * below[bit] == 0
+
     def spread(block, part, source):
         for bit in range(bits):
-            @pl.when(above[bit] == 0)
+            @pl.when(sends(bit, block, part))
             def _():
                 tree_copy(bit, block, part, source).start()
         for step in range(1, lanes):
@@ -171,6 +178,11 @@
         def _():
             spread(block, part, rows_ref.at[row_chunk(block, part)])
             cols_ref[col_chunk(lane, block, part)] = rows_ref[row_chunk(block, part)]
+
+        turned_ref[
+            pl.ds(pl.multiple_of(part * chunk_width, chunk_width), chunk_width),
+            pl.ds(pl.multiple_of(block * tokens, tokens), tokens),
+        ] = rows_ref[row_chunk(block, part)].T
 
     has_up = span < seq_devices - 1
     has_down = span > 0
@@ -203,7 +215,10 @@
                 weights.astype(jnp.bfloat16), values, preferred_element_type=jnp.float32
             )
             pieces.append((mixed / weight_sum).astype(jnp.bfloat16))
-        rows_ref[row_chunk(span, part)] = jnp.concatenate(pieces, axis=1)
+        joined = jnp.concatenate(pieces, axis=1)
+        rows_ref[row_chunk(span, part)] = joined
+        attended_ref[:, pl.ds(pl.multiple_of(part * chunk_width, chunk_width), chunk_width)] = joined
+
         on_row(span, part, has_up, has_down)
         return carry
 
@@ -225,24 +240,26 @@
             line_copy(1, block, part).wait_recv()
             on_row(block, part, False, has_down)
 
-        def from_parent(block):
-            source = cols_ref.at[col_chunk(lane, block, part)]
-            tree_copy(0, block, part, source).wait_recv()
-            spread(block, part, source)
-
-        @pl.when(not_root)
-        def _():
-            @pl.when(back <= span)
+        @pl.when(jnp.logical_and(not_root, item >= chunks))
+        def _():
+            late = back - 1
+
+            def from_parent(block):
+                source = cols_ref.at[col_chunk(lane, block, part)]
+                tree_copy(0, block, part, source).wait_recv()
+                spread(block, part, source)
+
+            @pl.when(late <= span)
             def _():
-                from_parent(span - back)
-
-            @pl.when(jnp.logical_and(back > 0, span + back < seq_devices))
+                from_parent(span - late)
+
+            @pl.when(jnp.logical_and(late > 0, span + late < seq_devices))
             def _():
-                from_parent(span + back)
+                from_parent(span + late)
 
         return carry
 
-    lax.fori_loop(0, seq_devices * chunks, relay, 0)
+    lax.fori_loop(0, (seq_devices + 1) * chunks, relay, 0)
 
     def drain(item, carry):
         block, part = item // chunks, item % chunks
@@ -257,7 +274,7 @@
             line_copy(1, block, part).wait_send()
 
         for bit in range(bits):
-            @pl.when(above[bit] == 0)
+            @pl.when(sends(bit, block, part))
             def _():
                 tree_copy(bit, block, part, source).wait_send()
         for step in range(1, lanes):
@@ -266,9 +283,18 @@
         return carry
 
     lax.fori_loop(0, seq_devices * chunks, drain, 0)
+
     for step in range(1, SPANS):
         for copy in kv_copies(step):
             copy.wait_send()
+
+
+def hessian_kernel(own_ref, turned_ref, cols_ref, attended_ref, out_ref):
+    @pl.when(pl.program_id(0) == 0)
+    def _():
+        attended_ref[...] = own_ref[...]
+
+    out_ref[...] = jnp.dot(turned_ref[...], cols_ref[...], preferred_element_type=jnp.float32)
 
 
 def on_device(query_rows, key_rows, value_rows, positions):
@@ -277,18 +303,20 @@
     head_devices = lax.axis_size("head")
     lanes = head_devices // seq_devices
     bits = seq_devices.bit_length() - 1
-    chunks = max(1, width // (4 * HD))
+    chunks = max(1, width // (CHUNK_HEADS * HD))
     vmem = pl.BlockSpec(memory_space=pltpu.VMEM)
     dma = pltpu.SemaphoreType.DMA
-    rows, cols = pl.pallas_call(
+    own, turned, cols = pl.pallas_call(
         functools.partial(exchange_kernel, seq_devices, head_devices, chunks),
         out_shape=(
-            jax.ShapeDtypeStruct((seq_devices * tokens, width), jnp.bfloat16),
+            jax.ShapeDtypeStruct((tokens, width), jnp.bfloat16),
+            jax.ShapeDtypeStruct((width, seq_devices * tokens), jnp.bfloat16),
             jax.ShapeDtypeStruct((seq_devices * tokens, lanes * width), jnp.bfloat16),
         ),
         in_specs=[vmem] * 4,
-        out_specs=(vmem, vmem),
+        out_specs=(vmem, vmem, vmem),
         scratch_shapes=[
+            pltpu.VMEM((seq_devices * tokens, width), jnp.bfloat16),
             pltpu.VMEM((SPANS, tokens, HD), jnp.bfloat16),
             pltpu.VMEM((SPANS, tokens, HD), jnp.bfloat16),
             pltpu.VMEM((SPANS, 1, tokens), jnp.int32),
@@ -304,10 +332,26 @@
         compiler_params=pltpu.CompilerParams(collective_id=0, has_side_effects=True),
         name="attend_exchange",
     )(query_rows, key_rows, value_rows, positions.reshape(1, tokens))
-    attended = lax.dynamic_slice_in_dim(rows, lax.axis_index("seq") * tokens, tokens, 0)
-    hessian = lax.dot_general(
-        rows, cols, (((0,), (0,)), ((), ())), preferred_element_type=jnp.float32
-    )
+    depth, breadth = cols.shape
+    tile = min(TILE, breadth)
+    attended, hessian = pl.pallas_call(
+        hessian_kernel,
+        grid=(breadth // tile,),
+        out_shape=(
+            jax.ShapeDtypeStruct((tokens, width), jnp.bfloat16),
+            jax.ShapeDtypeStruct((width, breadth), jnp.float32),
+        ),
+        in_specs=[
+            pl.BlockSpec((tokens, width), lambda j: (0, 0)),
+            pl.BlockSpec((width, depth), lambda j: (0, 0)),
+            pl.BlockSpec((depth, tile), lambda j: (0, j)),
+        ],
+        out_specs=(
+            pl.BlockSpec((tokens, width), lambda j: (0, 0)),
+            pl.BlockSpec((width, tile), lambda j: (0, j)),
+        ),
+        name="hessian",
+    )(own, turned, cols)
     return (attended, hessian)
 
 

time: 90.3 us -> 84.6 us (0.937)
  matrix products: 18.8 us -> 0 us
  Pallas kernels: 68.3 us -> 83.7 us
  local copies, waits for them, and re-layouts: 1.89 us -> 0 us
    dot_general x1 -> x0, matrix products: 18.8 us -> none  [on_device(): lax.dot_general(rows, cols, (((0,), (0,)), ((), ())), preferred_element_t...]
    pallas_call x0 -> x1, Pallas kernels: none -> 16.4 us  [on_device(): pl.pallas_call(hessian_kernel, grid=(breadth // tile,), out_shape=(jax.Sh...]
    dynamic_slice x1 -> x0, local copies, waits for them, and re-layouts: 1.89 us -> none  [on_device(): lax.dynamic_slice_in_dim(rows, lax.axis_index('seq') * tokens, tokens, 0)]
    pallas_call x1, Pallas kernels: 68.3 us -> 67.4 us  [on_device(): pl.pallas_call(functools.partial(exchange_kernel, seq_devices, head_devic...]
where the time goes in v2:
time: 84.6 us; the launch traced here: 84.4 us
  Pallas kernels  83.7 us (99%)
    pallas_call x1, Pallas kernels, on_device(): pl.pallas_call(functools.partial(exchange_kernel, seq_devices, head_devic...  67.4 us
    pallas_call x1, Pallas kernels, on_device(): pl.pallas_call(hessian_kernel, grid=(breadth // tile,), out_shape=(jax.Sh...  16.4 us

profile of v2, /device:TPU:25, one launch (start us, length us, event | category | flops | bytes accessed | tf_op | source)
XLA Modules:
  0.0 84.4 jit_solution(6724036176352421750)
XLA Ops:
  0.6 67.4 %attend_exchange.1 = (bf16[128,2048]{1,0:T(8,128)(2,1)}, bf16[2048,512]{1,0:T(8,128)(2,1)}, bf16[512,4096]{1,0:T(8,128)(2,1)}) custom-call(bf16[128,2048]{1,0:T(8,128)(2,1)} %q_ref.1, bf16[128,1024]{1,0:T(8,128)(2,1)} %k_ref.1, bf16[128,1024]{1,0:T(8,128)(2,1)} %v_ref.1, s32[1,128]{1,0:T(1,128)} %bitcast.1), custom_call_target="tpu_custom_call" | custom-call | tf_op jit(solution)/shard_map/attend_exchange/pallas_call | solution.py:309
  68.0 16.4 %hessian.1 = (bf16[128,2048]{1,0:T(8,128)(2,1)}, f32[2048,4096]{1,0:T(8,128)}) custom-call(bf16[128,2048]{1,0:T(8,128)(2,1)} %get-tuple-element.5.own_ref, bf16[2048,512]{1,0:T(8,128)(2,1)} %get-tuple-element.6.turned_ref, bf16[512,4096]{1,0:T(8,128)(2,1)} %get-tuple-element.7.cols_ref), custom_call_target="tpu_custom_call" | custom-call | tf_op jit(solution)/shard_map/hessian/pallas_call | solution.py:337
